TPU v7x, 512 devices: a whole 4x8x8 slice. The times are simulated.
512 devices in a mesh: atoms: 32 (over z, x), modes: 16 (over y, core).
Axes of the slice: x: 4, y: 8, z: 8, core: 2. Of those that a mesh axis runs over, the one named last changes fastest.
Arguments:
- subspace: float32 [768, 65536], P('modes', 'atoms'), may hold values from -100 to 100
- applied: float32 [768, 65536], P('modes', 'atoms'), may hold values from -300 to 300
Outputs:
- ortho_basis: float32 [768, 65536], P('modes', 'atoms')
- projected: float32 [768, 768], P('modes')
All inputs are finite; a program needn't handle non-finite values.
Results may differ from a plain program's by a relative error of at most 0.00025.
Values sent between devices are 32-bit elements; how exact they have to be, the bound alone decides.
A program may use at most 64 MiB of HBM per device.

v0:
```python
import jax
import jax.numpy as jnp
from jax import lax
from jax.experimental import pallas as pl
from jax.experimental.pallas import tpu as pltpu
from jax.sharding import PartitionSpec as P

MESH = pl.DeviceIdType.MESH
NX, NY, NZ = 4, 8, 8
GT, CT = 7, 9

B = 128
PANEL, STRIP = 32, 16
HI = lax.Precision.HIGHEST


def lane_bcast(v, j):
    return jnp.broadcast_to(v[:, j : j + 1], v.shape)


def row_bcast(v, j):
    return jnp.broadcast_to(v[j : j + 1, :], v.shape)


def factor_block(d_ref, m_ref):
    lane = lax.broadcasted_iota(jnp.int32, (8, B), 1)
    sub = lax.broadcasted_iota(jnp.int32, (8, B), 0)
    for s in range(B // 8):
        m_ref[8 * s : 8 * s + 8, :] = jnp.where(lane == sub + 8 * s, 1.0, 0.0)
    n = PANEL // 8
    for p0 in range(0, B, PANEL):
        d = [d_ref[p0 + 8 * g : p0 + 8 * g + 8, :] for g in range(n)]
        m = [m_ref[p0 + 8 * g : p0 + 8 * g + 8, :] for g in range(n)]
        for s0 in range(0, n, STRIP // 8):
            r0 = p0 + 8 * s0
            col = {g: [lane_bcast(d[g], r0 + k) for k in range(STRIP)] for g in range(s0, n)}
            scale = {}
            for j in range(STRIP):
                s, jj = s0 + j // 8, j % 8
                pivot = row_bcast(col[s][j], jj)
                inv = 1.0 / pivot
                root = lax.rsqrt(pivot)
                scale[s] = root if jj == 0 else jnp.where(sub >= jj, root, scale[s])
                dj = row_bcast(d[s], jj) * inv
                mj = row_bcast(m[s], jj) * inv
                for k in range(j + 1, STRIP):
                    f = row_bcast(col[s][k], jj) * inv
                    for g in range(s, n):
                        if g > s or jj < 7:
                            col[g][k] = col[g][k] - col[g][j] * f
                for g in range(s, n):
                    c = col[g][j]
                    if g == s:
                        if jj == 7:
                            continue
                        c = jnp.where(sub > jj, c, 0.0)
                    d[g] = d[g] - c * dj
                    m[g] = m[g] - c * mj
            for s in range(s0, s0 + STRIP // 8):
                d[s] = d[s] * scale[s]
                m[s] = m[s] * scale[s]
        for g in range(n):
            m_ref[p0 + 8 * g : p0 + 8 * g + 8, :] = m[g]
        if p0 + PANEL < B:
            r = jnp.concatenate(d, axis=0)
            q = jnp.concatenate(m, axis=0)
            t = r.T[p0 + PANEL :, :]
            d_ref[p0 + PANEL :, :] -= dot(t, r, ((1,), (0,)))
            m_ref[p0 + PANEL :, :] -= dot(t, q, ((1,), (0,)))


def dot(a, b, dims):
    return lax.dot_general(a, b, (dims, ((), ())), precision=HI, preferred_element_type=jnp.float32)


def dot3(a, b, dims):
    bf, f32 = jnp.bfloat16, jnp.float32
    ah, bh = a.astype(bf), b.astype(bf)
    al, bl = (a - ah.astype(f32)).astype(bf), (b - bh.astype(f32)).astype(bf)

    def one(p, q):
        return lax.dot_general(p, q, (dims, ((), ())), preferred_element_type=f32)

    return one(ah, bh) + (one(al, bh) + one(ah, bl))


def invert_lower(z_ref, d_ref, m_ref, between):
    n = z_ref.shape[0]
    steps = n // B
    row = lax.broadcasted_iota(jnp.int32, (B, B), 0)
    lane = lax.broadcasted_iota(jnp.int32, (B, B), 1)

    @pl.loop(0, steps)
    def _(k):
        between(k)
        k0 = pl.multiple_of(k * B, B)
        d = z_ref[pl.ds(k0, B), pl.ds(k0, B)]
        d_ref[...] = jnp.where(row >= lane, d, d.T)
        factor_block(d_ref, m_ref)
        for kk in range(steps):

            @pl.when(k == kk)
            def _():
                lo, hi = kk * B, (kk + 1) * B
                m = m_ref[...]
                if hi < n:
                    r = dot(m, z_ref[hi:, lo:hi], ((1,), (1,)))
                    rt = r.T
                    for c in range(hi, n, 2 * B):
                        e = min(c + 2 * B, n)
                        z_ref[c:, c:e] -= dot(rt[c - hi :], r[:, c - hi : e - hi], ((1,), (0,)))
                    z_ref[hi:, lo:hi] = jnp.zeros((n - hi, B), jnp.float32)
                    z_ref[lo:hi, hi:] = jnp.zeros((B, n - hi), jnp.float32)
                if kk:
                    z_ref[lo:hi, :lo] = dot(m, z_ref[lo:hi, :lo], ((1,), (0,)))
                z_ref[lo:hi, lo:hi] = m
                if hi < n:
                    z_ref[hi:, :hi] -= dot(rt, z_ref[lo:hi, :hi], ((1,), (0,)))


def copy_to(src, dst, send, recv, device):
    return pltpu.make_async_remote_copy(
        src_ref=src, dst_ref=dst, send_sem=send, recv_sem=recv, device_id=device, device_id_type=MESH
    )


class Exchange:
    def __init__(self, out, arriving):
        self.out, self.arriving = out, arriving

    def start(self):
        for c in self.out():
            c.start()

    def arrive(self):
        for c in self.arriving():
            c.wait_recv()

    def sent(self):
        for c in self.out():
            c.wait_send()


def kernel(
    s_hbm, a_hbm, ortho_ref, proj_ref,
    s_all, a_own, g_part, g_x, g_z, g_all, c_part, c_x, c_z, c_all, z_ref, ct_ref, d_ref, m_ref,
    load_sem, ring_send, ring_recv, twin_send, twin_recv, *sems,
):
    atom, mode = lax.axis_index("atoms"), lax.axis_index("modes")
    z, x = atom // NX, atom % NX
    y, core = mode // 2, mode % 2
    rows, wide = s_hbm.shape
    half_rows = rows // 2
    chip_rows = 2 * rows
    total = wide * NX * NZ

    def at_x(d):
        return (z * NX + (x + d) % NX, mode)

    def at_y(d):
        return (atom, ((y + d) % NY) * 2 + core)

    def at_z(d):
        return (((z + d) % NZ) * NX + x, mode)

    twin = (atom, y * 2 + (1 - core))

    barrier = pltpu.get_barrier_semaphore()
    peers = [at_z(d) for d in range(1, NZ)] + [at_y(d) for d in range(1, NY)]
    peers += [at_x(d) for d in range(1, NX)] + [twin]
    for peer in peers:
        pl.semaphore_signal(barrier, inc=1, device_id=peer, device_id_type=MESH)
    own_s = pltpu.make_async_copy(
        s_hbm, s_all.at[pl.ds(pl.multiple_of(mode * rows, 8), rows), :], load_sem.at[0]
    )
    own_a = pltpu.make_async_copy(a_hbm, a_own, load_sem.at[1])
    own_s.start()
    own_a.start()
    own_s.wait()
    pl.semaphore_wait(barrier, len(peers))

    pending = []

    def go(copy):
        copy.start()
        pending.append(copy)

    def piece(back, which, q):
        start = (((y + NY - back) % NY) * 2 + which) * rows + q * half_rows
        return s_all.at[pl.ds(pl.multiple_of(start, 8), half_rows), :]

    def ring(way, hop, q, back):
        ref = piece(back, core, q)
        sems = ring_send.at[way, hop, q], ring_recv.at[way, hop, q]
        return copy_to(ref, ref, *sems, at_y(1 if way == 0 else NY - 1))

    def ring_out(way, hop, q):
        return ring(way, hop, q, hop if way == 0 else (NY - hop) % NY)

    def ring_in(way, hop, q):
        return ring(way, hop, q, hop + 1 if way == 0 else NY - hop - 1)

    def to_twin(back, q, which):
        ref = piece(back, which, q)
        return copy_to(ref, ref, twin_send.at[back, q], twin_recv.at[back, q], twin)

    def pass_on(hop):
        for q in range(2):
            for way in range(2):
                ring_in(way, hop - 1, q).wait_recv()
                if hop < 3 or q == way:
                    go(ring_out(way, hop, q))
                go(to_twin(hop if way == 0 else NY - hop, q, core))

    def from_twin(*backs):
        for back in backs:
            for q in range(2):
                to_twin(back, q, 1 - core).wait_recv()

    for q in range(2):
        for way in range(2):
            go(ring_out(way, 0, q))
    for q in range(2):
        go(to_twin(0, q, core))
    pass_on(1)
    pass_on(2)
    from_twin(0, 1, 7, 2, 6)

    step = 256

    def chip_block(at, start, count, k):
        first = pl.multiple_of((at % NY) * chip_rows + start, 8)
        return s_all[pl.ds(first, count), k]

    far = (y + 2) % 4
    strip = chip_rows // 4

    def gram_step(i, acc):
        k = pl.ds(pl.multiple_of(i * step, 128), step)
        cols = chip_block(y + NY - core, 0, chip_rows, k)
        one = dot(chip_block(y + core, 0, chip_rows, k), cols, ((1,), (1,)))
        two = dot(chip_block(y + core + 1, 0, chip_rows, k), cols, ((1,), (1,)))
        edge = chip_block(far + 4, strip * (2 * (y // 4) + core), strip, k)
        three = dot(edge, chip_block(far, 0, chip_rows, k), ((1,), (1,)))
        return acc[0] + one, acc[1] + two, acc[2] + three

    nothing = jnp.zeros((chip_rows, chip_rows), jnp.float32)
    sums = lax.fori_loop(0, wide // step, gram_step, (nothing, nothing, nothing[:strip]))
    g_part[NX - 1, GT - 1] = jnp.zeros((8, 128), jnp.float32)
    t = 0
    for value in sums:
        for r in range(0, value.shape[0], 8):
            g_part[t // GT, t % GT, :, :chip_rows] = value[r : r + 8]
            t += 1

    def stages(sems, part, landing, spread, place):
        xs, xr, zs, zr, ys, yr, gs, gr, ts, tr = sems

        def x_copies():
            return [
                copy_to(part.at[(x + d) % NX], landing.at[d - 1], xs.at[d - 1], xr.at[d - 1], at_x(d))
                for d in range(1, NX)
            ]

        def x_total():
            spread[z] = (part[x] + landing[0] + landing[1] + landing[2]) * (1.0 / total)

        def z_copies(sign):
            def make():
                refs = [spread.at[(z + sign * d + NZ) % NZ if sign else z] for d in range(1, NZ)]
                return [copy_to(r, r, zs.at[d], zr.at[d], at_z(d + 1)) for d, r in enumerate(refs)]

            return make

        def z_total():
            value = spread[0]
            for i in range(1, NZ):
                value = value + spread[i]
            place[core, y, x] = value

        def y_copies(sign):
            def make():
                refs = [place.at[core, (y + sign * d + NY) % NY, x] for d in range(1, NY)]
                return [copy_to(r, r, ys.at[d], yr.at[d], at_y(d + 1)) for d, r in enumerate(refs)]

            return make

        def g_copies(sign):
            def make():
                refs = [place.at[core, :, (x + sign * d + NX) % NX] for d in range(1, NX)]
                return [copy_to(r, r, gs.at[d], gr.at[d], at_x(d + 1)) for d, r in enumerate(refs)]

            return make

        def t_copies(which):
            def make():
                return [copy_to(place.at[which], place.at[which], ts.at[0], tr.at[0], twin)]

            return make

        return (
            Exchange(x_copies, x_copies), x_total,
            Exchange(z_copies(0), z_copies(-1)), z_total,
            Exchange(y_copies(0), y_copies(-1)),
            Exchange(g_copies(0), g_copies(-1)),
            Exchange(t_copies(core), t_copies(1 - core)),
        )

    gx, gx_total, gz, gz_total, gy, gg, gt = stages(sems[:10], g_part, g_x, g_z, g_all)
    cx, cx_total, cz, cz_total, cy, cg, ct = stages(sems[10:], c_part, c_x, c_z, c_all)

    gx.start()
    gx.arrive()
    gx_total()
    gz.start()
    pass_on(3)
    for way in range(2):
        ring_in(way, 3, way).wait_recv()
        go(to_twin(4, way, core))
    gz.arrive()
    gz_total()
    gy.start()
    own_a.wait()
    from_twin(5, 3, 4)

    def cross_step(i, acc):
        k = pl.ds(pl.multiple_of(i * step, 128), step)
        return acc + dot3(a_own[:, k], s_all[:, k], ((1,), (1,)))

    crosst = lax.fori_loop(0, wide // step, cross_step, jnp.zeros((rows, s_all.shape[0]), jnp.float32))
    for t in range(NX * CT):
        r, h = 8 * (t // 6), 128 * (t % 6)
        c_part[t // CT, t % CT] = crosst[r : r + 8, h : h + 128]
    cx.start()
    gy.arrive()
    gg.start()
    cx.arrive()
    cx_total()
    cz.start()
    gg.arrive()
    gt.start()
    gt.arrive()

    for chip in range(NY):
        for which in range(2):
            tiles = [g_all[which, chip, t // GT, t % GT][:, :chip_rows] for t in range(NX * GT - 1)]
            blocks = chip_rows // 8
            for b in range(2):
                at, col = (chip + which + b) % NY, (chip - which) % NY
                block = tiles[b * blocks : (b + 1) * blocks]
                if at < col:
                    flipped = jnp.concatenate(block, axis=0).T
                    block = [flipped[8 * r : 8 * r + 8] for r in range(blocks)]
                    at, col = col, at
                for r, tile in enumerate(block):
                    first = at * chip_rows + 8 * r
                    z_ref[first : first + 8, col * chip_rows : (col + 1) * chip_rows] = tile
            col = (chip + 2) % 4
            for r, tile in enumerate(tiles[2 * blocks :]):
                first = (col + 4) * chip_rows + strip * (2 * (chip // 4) + which) + 8 * r
                z_ref[first : first + 8, col * chip_rows : (col + 1) * chip_rows] = tile

    def between(k):
        @pl.when(k == 1)
        def _():
            cz.arrive()
            cz_total()
            cy.start()

        @pl.when(k == 3)
        def _():
            cy.arrive()
            cg.start()

        @pl.when(k == 5)
        def _():
            cg.arrive()
            ct.start()

    invert_lower(z_ref, d_ref, m_ref, between)

    lower = z_ref[pl.ds(pl.multiple_of(mode * rows, 8), rows), :]

    @pl.loop(0, wide // step)
    def _(i):
        k = pl.ds(pl.multiple_of(i * step, 128), step)
        ortho_ref[:, k] = dot3(lower, s_all[:, k], ((1,), (0,)))

    ct.arrive()
    for m in range(2 * NY):
        for t in range(NX * CT):
            r, h = m * rows + 8 * (t // 6), 128 * (t % 6)
            ct_ref[r : r + 8, h : h + 128] = c_all[m % 2, m // 2, t // CT, t % CT]
    half = dot3(lower, ct_ref[...], ((1,), (1,)))
    proj_ref[...] = dot3(half, z_ref[...], ((1,), (1,)))
    for c in pending:
        c.wait_send()
    for e in (gx, gz, gy, gg, gt, cx, cz, cy, cg, ct):
        e.sent()


def per_device(subspace, applied):
    rows, wide = subspace.shape
    n = rows * lax.axis_size("modes")
    f32 = jnp.float32
    dma = pltpu.SemaphoreType.DMA
    exchange = [dma((count,)) for count in (NX - 1, NZ - 1, NY - 1, NX - 1, 1) for _ in range(2)]

    def buffers(count):
        return [
            pltpu.VMEM((NX, count, 8, 128), f32),
            pltpu.VMEM((NX - 1, count, 8, 128), f32),
            pltpu.VMEM((NZ, count, 8, 128), f32),
            pltpu.VMEM((2, NY, NX, count, 8, 128), f32),
        ]

    return pl.pallas_call(
        kernel,
        out_shape=(
            jax.ShapeDtypeStruct((rows, wide), f32),
            jax.ShapeDtypeStruct((rows, n), f32),
        ),
        in_specs=[pl.BlockSpec(memory_space=pl.ANY)] * 2,
        out_specs=[pl.BlockSpec(memory_space=pltpu.VMEM)] * 2,
        scratch_shapes=[
            pltpu.VMEM((n, wide), f32),
            pltpu.VMEM((rows, wide), f32),
            *buffers(GT),
            *buffers(CT),
            pltpu.VMEM((n, n), f32),
            pltpu.VMEM((n, n), f32),
            pltpu.VMEM((B, B), f32),
            pltpu.VMEM((B, B), f32),
            dma((2,)),
            *[dma((2, 4, 2)) for _ in range(2)],
            *[dma((NY, 2)) for _ in range(2)],
            *exchange,
            *exchange,
        ],
        compiler_params=pltpu.CompilerParams(
            collective_id=0, has_side_effects=True, vmem_limit_bytes=56 * 2**20
        ),
        name="cholesky_qr",
    )(subspace, applied)


def solution(mesh):
    return jax.shard_map(
        per_device,
        mesh=mesh,
        in_specs=(P("modes", "atoms"), P("modes", "atoms")),
        out_specs=(P("modes", "atoms"), P("modes", None)),
        check_vma=False,
    )
```

profile of v0, /device:TPU:1, one launch (start us, length us, event | category | flops | bytes accessed | tf_op | source)
XLA Modules:
  0.0 119.2 jit_solution(13773751735958363936)
XLA Ops:
  0.6 116.1 %cholesky_qr.1 = (f32[48,2048]{1,0:T(8,128)}, f32[48,768]{1,0:T(8,128)}) custom-call(f32[48,2048]{1,0:T(8,128)} %s_hbm.1, f32[48,2048]{1,0:T(8,128)} %a_hbm.1), custom_call_target="tpu_custom_call" | custom-call | tf_op jit(solution)/shard_map/cholesky_qr/pallas_call | solution.py:417
  116.7 0.0 copy-start
  116.7 1.8 %copy.6 = f32[48,2048]{1,0:T(8,128)} copy(f32[48,2048]{1,0:T(8,128)} %get-tuple-element.4) | data formatting | bytes 786432
  118.5 0.0 copy-done
  118.5 0.7 copy.7
Async XLA Ops:
  116.7 1.8 %copy-start = (f32[48,768]{1,0:T(8,128)S(1)}, f32[48,768]{1,0:T(8,128)}, u32[]{:S(2)}) copy-start(f32[48,768]{1,0:T(8,128)} %get-tuple-element.5) | copy-start | bytes 442372
where the time goes:
time: 119 us
  Pallas kernels  116 us (97%)
  local copies, waits for them, and re-layouts  2.47 us (2%)
    pallas_call x1, Pallas kernels, per_device(): pl.pallas_call(kernel, out_shape=(jax.ShapeDtypeStruct((rows, wide), f32)...  116 us
    unnamed x4, local copies, waits for them, and re-layouts  2.47 us

commit v1 on v0

--- a/solution.py
+++ b/solution.py
@@ -86,42 +86,106 @@
 
 def invert_lower(z_ref, d_ref, m_ref, between):
     n = z_ref.shape[0]
-    steps = n // B
     row = lax.broadcasted_iota(jnp.int32, (B, B), 0)
     lane = lax.broadcasted_iota(jnp.int32, (B, B), 1)
 
-    @pl.loop(0, steps)
-    def _(k):
+    def inverse_of_block(k):
+        d = z_ref[k * B : (k + 1) * B, k * B : (k + 1) * B]
+        d_ref[k] = jnp.where(row >= lane, d, d.T)
+        factor_block(d_ref.at[k], m_ref.at[k])
+        return m_ref[k]
+
+    following = inverse_of_block(0)
+    for k in range(n // B):
         between(k)
-        k0 = pl.multiple_of(k * B, B)
-        d = z_ref[pl.ds(k0, B), pl.ds(k0, B)]
-        d_ref[...] = jnp.where(row >= lane, d, d.T)
-        factor_block(d_ref, m_ref)
-        for kk in range(steps):
-
-            @pl.when(k == kk)
-            def _():
-                lo, hi = kk * B, (kk + 1) * B
-                m = m_ref[...]
-                if hi < n:
-                    r = dot(m, z_ref[hi:, lo:hi], ((1,), (1,)))
-                    rt = r.T
-                    for c in range(hi, n, 2 * B):
-                        e = min(c + 2 * B, n)
-                        z_ref[c:, c:e] -= dot(rt[c - hi :], r[:, c - hi : e - hi], ((1,), (0,)))
-                    z_ref[hi:, lo:hi] = jnp.zeros((n - hi, B), jnp.float32)
-                    z_ref[lo:hi, hi:] = jnp.zeros((B, n - hi), jnp.float32)
-                if kk:
-                    z_ref[lo:hi, :lo] = dot(m, z_ref[lo:hi, :lo], ((1,), (0,)))
-                z_ref[lo:hi, lo:hi] = m
-                if hi < n:
-                    z_ref[hi:, :hi] -= dot(rt, z_ref[lo:hi, :hi], ((1,), (0,)))
+        lo, hi = k * B, (k + 1) * B
+        m = following
+        if hi < n:
+            r = dot(m, z_ref[hi:, lo:hi], ((1,), (1,)))
+            rt = r.T
+            z_ref[hi : hi + B, hi : hi + B] -= dot(rt[:B], r[:, :B], ((1,), (0,)))
+            following = inverse_of_block(k + 1)
+            if hi + B < n:
+                z_ref[hi + B :, hi : hi + B] -= dot(rt[B:], r[:, :B], ((1,), (0,)))
+            for c in range(hi + B, n, 2 * B):
+                e = min(c + 2 * B, n)
+                z_ref[c:, c:e] -= dot(rt[c - hi :], r[:, c - hi : e - hi], ((1,), (0,)))
+            z_ref[lo:hi, hi:] = jnp.zeros((B, n - hi), jnp.float32)
+        if k:
+            w = dot(m, z_ref[lo:hi, :lo], ((1,), (0,)))
+            z_ref[lo:hi, :lo] = w
+            if hi < n:
+                z_ref[hi:, :lo] -= dot(rt, w, ((1,), (0,)))
+        z_ref[lo:hi, lo:hi] = m
+        if hi < n:
+            z_ref[hi:, lo:hi] = -dot(rt, m, ((1,), (0,)))
 
 
 def copy_to(src, dst, send, recv, device):
     return pltpu.make_async_remote_copy(
         src_ref=src, dst_ref=dst, send_sem=send, recv_sem=recv, device_id=device, device_id_type=MESH
     )
+
+
+class Spread:
+    def __init__(self, place, sems, me, at_x, at_y, twin):
+        self.place, self.sems, self.me = place, sems, me
+        self.at_x, self.at_y, self.twin = at_x, at_y, twin
+
+    def part(self, back_y, back_x, other=False):
+        core, y, x = self.me
+        which = 1 - core if other else core
+        return self.place.at[which, (y + NY - back_y) % NY, (x + NX - back_x) % NX]
+
+    def along_y(self, d, arriving=False):
+        ys, yr = self.sems[:2]
+        ref = self.part(d if arriving else 0, 0)
+        return copy_to(ref, ref, ys.at[d - 1], yr.at[d - 1], self.at_y(d))
+
+    def along_x(self, back_y, d, arriving=False):
+        xs, xr = self.sems[2:4]
+        ref = self.part(back_y, d if arriving else 0)
+        return copy_to(ref, ref, xs.at[back_y, d - 1], xr.at[back_y, d - 1], self.at_x(d))
+
+    def to_twin(self, back_y, back_x, arriving=False):
+        ts, tr = self.sems[4:]
+        ref = self.part(back_y, back_x, arriving)
+        return copy_to(ref, ref, ts.at[back_y, back_x], tr.at[back_y, back_x], self.twin)
+
+    def pass_on(self, back_y):
+        for d in range(1, NX):
+            self.along_x(back_y, d).start()
+        self.to_twin(back_y, 0).start()
+
+    def start(self):
+        for d in range(1, NY):
+            self.along_y(d).start()
+        self.pass_on(0)
+
+    def forward(self, *backs):
+        for back in backs:
+            self.along_y(back, arriving=True).wait_recv()
+            self.pass_on(back)
+
+    def collect(self, *backs):
+        for back in backs:
+            for d in range(1, NX):
+                self.along_x(back, d, arriving=True).wait_recv()
+                self.to_twin(back, d).start()
+
+    def arrive(self):
+        for back_y in range(NY):
+            for back_x in range(NX):
+                self.to_twin(back_y, back_x, arriving=True).wait_recv()
+
+    def sent(self):
+        for d in range(1, NY):
+            self.along_y(d).wait_send()
+        for back_y in range(NY):
+            for d in range(1, NX):
+                self.along_x(back_y, d).wait_send()
+            for back_x in range(NX):
+                self.to_twin(back_y, back_x).wait_send()
 
 
 class Exchange:
@@ -238,14 +302,14 @@
     def gram_step(i, acc):
         k = pl.ds(pl.multiple_of(i * step, 128), step)
         cols = chip_block(y + NY - core, 0, chip_rows, k)
-        one = dot(chip_block(y + core, 0, chip_rows, k), cols, ((1,), (1,)))
-        two = dot(chip_block(y + core + 1, 0, chip_rows, k), cols, ((1,), (1,)))
+        both = [chip_block(y + core + b, 0, chip_rows, k) for b in range(2)]
+        main = dot(jnp.concatenate(both, axis=0), cols, ((1,), (1,)))
         edge = chip_block(far + 4, strip * (2 * (y // 4) + core), strip, k)
-        three = dot(edge, chip_block(far, 0, chip_rows, k), ((1,), (1,)))
-        return acc[0] + one, acc[1] + two, acc[2] + three
-
-    nothing = jnp.zeros((chip_rows, chip_rows), jnp.float32)
-    sums = lax.fori_loop(0, wide // step, gram_step, (nothing, nothing, nothing[:strip]))
+        side = dot(edge, chip_block(far, 0, chip_rows, k), ((1,), (1,)))
+        return acc[0] + main, acc[1] + side
+
+    nothing = jnp.zeros((2 * chip_rows, chip_rows), jnp.float32)
+    sums = lax.fori_loop(0, wide // step, gram_step, (nothing, nothing[:strip]), unroll=2)
     g_part[NX - 1, GT - 1] = jnp.zeros((8, 128), jnp.float32)
     t = 0
     for value in sums:
@@ -254,7 +318,7 @@
             t += 1
 
     def stages(sems, part, landing, spread, place):
-        xs, xr, zs, zr, ys, yr, gs, gr, ts, tr = sems
+        xs, xr, zs, zr, *rest = sems
 
         def x_copies():
             return [
@@ -278,36 +342,14 @@
                 value = value + spread[i]
             place[core, y, x] = value
 
-        def y_copies(sign):
-            def make():
-                refs = [place.at[core, (y + sign * d + NY) % NY, x] for d in range(1, NY)]
-                return [copy_to(r, r, ys.at[d], yr.at[d], at_y(d + 1)) for d, r in enumerate(refs)]
-
-            return make
-
-        def g_copies(sign):
-            def make():
-                refs = [place.at[core, :, (x + sign * d + NX) % NX] for d in range(1, NX)]
-                return [copy_to(r, r, gs.at[d], gr.at[d], at_x(d + 1)) for d, r in enumerate(refs)]
-
-            return make
-
-        def t_copies(which):
-            def make():
-                return [copy_to(place.at[which], place.at[which], ts.at[0], tr.at[0], twin)]
-
-            return make
-
         return (
             Exchange(x_copies, x_copies), x_total,
             Exchange(z_copies(0), z_copies(-1)), z_total,
-            Exchange(y_copies(0), y_copies(-1)),
-            Exchange(g_copies(0), g_copies(-1)),
-            Exchange(t_copies(core), t_copies(1 - core)),
+            Spread(place, rest, (core, y, x), at_x, at_y, twin),
         )
 
-    gx, gx_total, gz, gz_total, gy, gg, gt = stages(sems[:10], g_part, g_x, g_z, g_all)
-    cx, cx_total, cz, cz_total, cy, cg, ct = stages(sems[10:], c_part, c_x, c_z, c_all)
+    gx, gx_total, gz, gz_total, g_spread = stages(sems[:10], g_part, g_x, g_z, g_all)
+    cx, cx_total, cz, cz_total, c_spread = stages(sems[10:], c_part, c_x, c_z, c_all)
 
     gx.start()
     gx.arrive()
@@ -319,7 +361,7 @@
         go(to_twin(4, way, core))
     gz.arrive()
     gz_total()
-    gy.start()
+    g_spread.start()
     own_a.wait()
     from_twin(5, 3, 4)
 
@@ -332,14 +374,12 @@
         r, h = 8 * (t // 6), 128 * (t % 6)
         c_part[t // CT, t % CT] = crosst[r : r + 8, h : h + 128]
     cx.start()
-    gy.arrive()
-    gg.start()
+    g_spread.forward(1, 7, 2, 6, 3, 5, 4)
     cx.arrive()
     cx_total()
     cz.start()
-    gg.arrive()
-    gt.start()
-    gt.arrive()
+    g_spread.collect(0, 1, 7, 2, 6, 3, 5, 4)
+    g_spread.arrive()
 
     for chip in range(NY):
         for which in range(2):
@@ -361,32 +401,27 @@
                 z_ref[first : first + 8, col * chip_rows : (col + 1) * chip_rows] = tile
 
     def between(k):
-        @pl.when(k == 1)
-        def _():
+        if k == 0:
             cz.arrive()
             cz_total()
-            cy.start()
-
-        @pl.when(k == 3)
-        def _():
-            cy.arrive()
-            cg.start()
-
-        @pl.when(k == 5)
-        def _():
-            cg.arrive()
-            ct.start()
+            c_spread.start()
+        if k == 1:
+            c_spread.forward(1, 7, 2, 6)
+        if k == 2:
+            c_spread.forward(3, 5, 4)
+        if k == 4:
+            c_spread.collect(0, 1, 7)
 
     invert_lower(z_ref, d_ref, m_ref, between)
 
     lower = z_ref[pl.ds(pl.multiple_of(mode * rows, 8), rows), :]
 
-    @pl.loop(0, wide // step)
-    def _(i):
-        k = pl.ds(pl.multiple_of(i * step, 128), step)
-        ortho_ref[:, k] = dot3(lower, s_all[:, k], ((1,), (0,)))
-
-    ct.arrive()
+    for i in range(0, wide, step):
+        ortho_ref[:, i : i + step] = dot3(lower, s_all[:, i : i + step], ((1,), (0,)))
+        if i == 0:
+            c_spread.collect(2, 6, 3, 5, 4)
+
+    c_spread.arrive()
     for m in range(2 * NY):
         for t in range(NX * CT):
             r, h = m * rows + 8 * (t // 6), 128 * (t % 6)
@@ -395,7 +430,7 @@
     proj_ref[...] = dot3(half, z_ref[...], ((1,), (1,)))
     for c in pending:
         c.wait_send()
-    for e in (gx, gz, gy, gg, gt, cx, cz, cy, cg, ct):
+    for e in (gx, gz, g_spread, cx, cz, c_spread):
         e.sent()
 
 
@@ -404,7 +439,8 @@
     n = rows * lax.axis_size("modes")
     f32 = jnp.float32
     dma = pltpu.SemaphoreType.DMA
-    exchange = [dma((count,)) for count in (NX - 1, NZ - 1, NY - 1, NX - 1, 1) for _ in range(2)]
+    shapes = ((NX - 1,), (NZ - 1,), (NY - 1,), (NY, NX - 1), (NY, NX))
+    exchange = [dma(shape) for shape in shapes for _ in range(2)]
 
     def buffers(count):
         return [
@@ -429,8 +465,8 @@
             *buffers(CT),
             pltpu.VMEM((n, n), f32),
             pltpu.VMEM((n, n), f32),
-            pltpu.VMEM((B, B), f32),
-            pltpu.VMEM((B, B), f32),
+            pltpu.VMEM((n // B, B, B), f32),
+            pltpu.VMEM((n // B, B, B), f32),
             dma((2,)),
             *[dma((2, 4, 2)) for _ in range(2)],
             *[dma((NY, 2)) for _ in range(2)],

time: 119 us -> 110 us (0.924)
  Pallas kernels: 116 us -> 107 us
    pallas_call x1, Pallas kernels: 116 us -> 107 us  [per_device(): pl.pallas_call(kernel, out_shape=(jax.ShapeDtypeStruct((rows, wide), f32)...]
where the time goes in v1:
time: 110 us
  Pallas kernels  107 us (97%)
  local copies, waits for them, and re-layouts  2.47 us (2%)
    pallas_call x1, Pallas kernels, per_device(): pl.pallas_call(kernel, out_shape=(jax.ShapeDtypeStruct((rows, wide), f32)...  107 us
    unnamed x4, local copies, waits for them, and re-layouts  2.47 us

profile of v1, /device:TPU:1, one launch (start us, length us, event | category | flops | bytes accessed | tf_op | source)
XLA Modules:
  0.0 109.9 jit_solution(10747578457433229823)
XLA Ops:
  0.6 106.8 %cholesky_qr.1 = (f32[48,2048]{1,0:T(8,128)}, f32[48,768]{1,0:T(8,128)}) custom-call(f32[48,2048]{1,0:T(8,128)} %s_hbm.1, f32[48,2048]{1,0:T(8,128)} %a_hbm.1), custom_call_target="tpu_custom_call" | custom-call | tf_op jit(solution)/shard_map/cholesky_qr/pallas_call | solution.py:453
  107.4 0.0 copy-start
  107.4 1.8 %copy.6 = f32[48,2048]{1,0:T(8,128)} copy(f32[48,2048]{1,0:T(8,128)} %get-tuple-element.4) | data formatting | bytes 786432
  109.3 0.0 copy-done
  109.3 0.7 copy.7
Async XLA Ops:
  107.4 1.8 %copy-start = (f32[48,768]{1,0:T(8,128)S(1)}, f32[48,768]{1,0:T(8,128)}, u32[]{:S(2)}) copy-start(f32[48,768]{1,0:T(8,128)} %get-tuple-element.5) | copy-start | bytes 442372

commit v2 on v1

--- a/solution.py
+++ b/solution.py
@@ -127,65 +127,70 @@
     )
 
 
+def slot_of(back):
+    over = back // (NY // 2 + 1)
+    return (1 - over) * (2 * back - (back + NY - 1) // NY) + over * 2 * (NY - back)
+
+
 class Spread:
+    GROUPS = (5, 3)
+
     def __init__(self, place, sems, me, at_x, at_y, twin):
         self.place, self.sems, self.me = place, sems, me
         self.at_x, self.at_y, self.twin = at_x, at_y, twin
 
-    def part(self, back_y, back_x, other=False):
-        core, y, x = self.me
-        which = 1 - core if other else core
-        return self.place.at[which, (y + NY - back_y) % NY, (x + NX - back_x) % NX]
-
     def along_y(self, d, arriving=False):
         ys, yr = self.sems[:2]
-        ref = self.part(d if arriving else 0, 0)
-        return copy_to(ref, ref, ys.at[d - 1], yr.at[d - 1], self.at_y(d))
-
-    def along_x(self, back_y, d, arriving=False):
+        core, _, x = self.me
+        return copy_to(
+            self.place.at[core, 0, x], self.place.at[core, slot_of(d), x], ys.at[d - 1], yr.at[d - 1], self.at_y(d)
+        )
+
+    def group(self, g, back_x, other=False):
+        core, _, x = self.me
+        which = 1 - core if other else core
+        slots = pl.ds(sum(self.GROUPS[:g]), self.GROUPS[g])
+        return self.place.at[which, slots, (x + NX - back_x) % NX]
+
+    def along_x(self, g, d, arriving=False):
         xs, xr = self.sems[2:4]
-        ref = self.part(back_y, d if arriving else 0)
-        return copy_to(ref, ref, xs.at[back_y, d - 1], xr.at[back_y, d - 1], self.at_x(d))
-
-    def to_twin(self, back_y, back_x, arriving=False):
+        ref = self.group(g, d if arriving else 0)
+        return copy_to(ref, ref, xs.at[g, d - 1], xr.at[g, d - 1], self.at_x(d))
+
+    def to_twin(self, g, back_x, arriving=False):
         ts, tr = self.sems[4:]
-        ref = self.part(back_y, back_x, arriving)
-        return copy_to(ref, ref, ts.at[back_y, back_x], tr.at[back_y, back_x], self.twin)
-
-    def pass_on(self, back_y):
-        for d in range(1, NX):
-            self.along_x(back_y, d).start()
-        self.to_twin(back_y, 0).start()
+        ref = self.group(g, back_x, arriving)
+        return copy_to(ref, ref, ts.at[g, back_x], tr.at[g, back_x], self.twin)
 
     def start(self):
-        for d in range(1, NY):
+        for d in (1, 7, 2, 6, 3, 5, 4):
             self.along_y(d).start()
-        self.pass_on(0)
-
-    def forward(self, *backs):
-        for back in backs:
-            self.along_y(back, arriving=True).wait_recv()
-            self.pass_on(back)
-
-    def collect(self, *backs):
-        for back in backs:
-            for d in range(1, NX):
-                self.along_x(back, d, arriving=True).wait_recv()
-                self.to_twin(back, d).start()
+
+    def forward(self, g):
+        for d in ((1, 7, 2, 6), (3, 5, 4))[g]:
+            self.along_y(d, arriving=True).wait_recv()
+        for d in (2, 1, 3):
+            self.along_x(g, d).start()
+        self.to_twin(g, 0).start()
+
+    def collect(self, g):
+        for d in (1, 3, 2):
+            self.along_x(g, d, arriving=True).wait_recv()
+            self.to_twin(g, d).start()
 
     def arrive(self):
-        for back_y in range(NY):
+        for g in range(2):
             for back_x in range(NX):
-                self.to_twin(back_y, back_x, arriving=True).wait_recv()
+                self.to_twin(g, back_x, arriving=True).wait_recv()
 
     def sent(self):
         for d in range(1, NY):
             self.along_y(d).wait_send()
-        for back_y in range(NY):
+        for g in range(2):
             for d in range(1, NX):
-                self.along_x(back_y, d).wait_send()
+                self.along_x(g, d).wait_send()
             for back_x in range(NX):
-                self.to_twin(back_y, back_x).wait_send()
+                self.to_twin(g, back_x).wait_send()
 
 
 class Exchange:
@@ -340,7 +345,7 @@
             value = spread[0]
             for i in range(1, NZ):
                 value = value + spread[i]
-            place[core, y, x] = value
+            place[core, 0, x] = value
 
         return (
             Exchange(x_copies, x_copies), x_total,
@@ -374,16 +379,22 @@
         r, h = 8 * (t // 6), 128 * (t % 6)
         c_part[t // CT, t % CT] = crosst[r : r + 8, h : h + 128]
     cx.start()
-    g_spread.forward(1, 7, 2, 6, 3, 5, 4)
+    g_spread.forward(0)
     cx.arrive()
     cx_total()
     cz.start()
-    g_spread.collect(0, 1, 7, 2, 6, 3, 5, 4)
+    g_spread.forward(1)
+    g_spread.collect(0)
+    g_spread.collect(1)
+    cz.arrive()
+    cz_total()
+    c_spread.start()
     g_spread.arrive()
 
+    slots = [slot_of((y + NY - chip) % NY) for chip in range(NY)]
     for chip in range(NY):
         for which in range(2):
-            tiles = [g_all[which, chip, t // GT, t % GT][:, :chip_rows] for t in range(NX * GT - 1)]
+            tiles = [g_all[which, slots[chip], t // GT, t % GT][:, :chip_rows] for t in range(NX * GT - 1)]
             blocks = chip_rows // 8
             for b in range(2):
                 at, col = (chip + which + b) % NY, (chip - which) % NY
@@ -401,16 +412,10 @@
                 z_ref[first : first + 8, col * chip_rows : (col + 1) * chip_rows] = tile
 
     def between(k):
-        if k == 0:
-            cz.arrive()
-            cz_total()
-            c_spread.start()
-        if k == 1:
-            c_spread.forward(1, 7, 2, 6)
-        if k == 2:
-            c_spread.forward(3, 5, 4)
-        if k == 4:
-            c_spread.collect(0, 1, 7)
+        if k < 2:
+            c_spread.forward(k)
+        elif k > 3:
+            c_spread.collect(k - 4)
 
     invert_lower(z_ref, d_ref, m_ref, between)
 
@@ -418,14 +423,12 @@
 
     for i in range(0, wide, step):
         ortho_ref[:, i : i + step] = dot3(lower, s_all[:, i : i + step], ((1,), (0,)))
-        if i == 0:
-            c_spread.collect(2, 6, 3, 5, 4)
 
     c_spread.arrive()
     for m in range(2 * NY):
         for t in range(NX * CT):
             r, h = m * rows + 8 * (t // 6), 128 * (t % 6)
-            ct_ref[r : r + 8, h : h + 128] = c_all[m % 2, m // 2, t // CT, t % CT]
+            ct_ref[r : r + 8, h : h + 128] = c_all[m % 2, slots[m // 2], t // CT, t % CT]
     half = dot3(lower, ct_ref[...], ((1,), (1,)))
     proj_ref[...] = dot3(half, z_ref[...], ((1,), (1,)))
     for c in pending:
@@ -439,7 +442,7 @@
     n = rows * lax.axis_size("modes")
     f32 = jnp.float32
     dma = pltpu.SemaphoreType.DMA
-    shapes = ((NX - 1,), (NZ - 1,), (NY - 1,), (NY, NX - 1), (NY, NX))
+    shapes = ((NX - 1,), (NZ - 1,), (NY - 1,), (2, NX - 1), (2, NX))
     exchange = [dma(shape) for shape in shapes for _ in range(2)]
 
     def buffers(count):

time: 110 us -> 107 us (0.973)
  Pallas kernels: 107 us -> 103 us
    pallas_call x1, Pallas kernels: 107 us -> 103 us  [per_device(): pl.pallas_call(kernel, out_shape=(jax.ShapeDtypeStruct((rows, wide), f32)...]
where the time goes in v2:
time: 107 us; the launch traced here: 106 us
  Pallas kernels  103 us (96%)
  local copies, waits for them, and re-layouts  2.47 us (2%)
    pallas_call x1, Pallas kernels, per_device(): pl.pallas_call(kernel, out_shape=(jax.ShapeDtypeStruct((rows, wide), f32)...  103 us
    unnamed x4, local copies, waits for them, and re-layouts  2.47 us

profile of v2, /device:TPU:1, one launch (start us, length us, event | category | flops | bytes accessed | tf_op | source)
XLA Modules:
  0.0 106.0 jit_solution(13052619687786428479)
XLA Ops:
  0.6 102.9 %cholesky_qr.1 = (f32[48,2048]{1,0:T(8,128)}, f32[48,768]{1,0:T(8,128)}) custom-call(f32[48,2048]{1,0:T(8,128)} %s_hbm.1, f32[48,2048]{1,0:T(8,128)} %a_hbm.1), custom_call_target="tpu_custom_call" | custom-call | tf_op jit(solution)/shard_map/cholesky_qr/pallas_call | solution.py:456
  103.5 0.0 copy-start
  103.5 1.8 %copy.6 = f32[48,2048]{1,0:T(8,128)} copy(f32[48,2048]{1,0:T(8,128)} %get-tuple-element.4) | data formatting | bytes 786432
  105.3 0.0 copy-done
  105.3 0.7 copy.7
Async XLA Ops:
  103.5 1.8 %copy-start = (f32[48,768]{1,0:T(8,128)S(1)}, f32[48,768]{1,0:T(8,128)}, u32[]{:S(2)}) copy-start(f32[48,768]{1,0:T(8,128)} %get-tuple-element.5) | copy-start | bytes 442372

commit v3 on v2

--- a/solution.py
+++ b/solution.py
@@ -198,8 +198,10 @@
         self.out, self.arriving = out, arriving
 
     def start(self):
-        for c in self.out():
-            c.start()
+        copies = self.out()
+        far = (len(copies) + 1) / 2
+        for i in sorted(range(len(copies)), key=lambda i: abs(i + 1 - far)):
+            copies[i].start()
 
     def arrive(self):
         for c in self.arriving():

time: 107 us -> 107 us (level)
  no operation moved by 1% of the time
where the time goes in v3:
time: 107 us
  Pallas kernels  103 us (96%)
  local copies, waits for them, and re-layouts  2.47 us (2%)
    pallas_call x1, Pallas kernels, per_device(): pl.pallas_call(kernel, out_shape=(jax.ShapeDtypeStruct((rows, wide), f32)...  103 us
    unnamed x4, local copies, waits for them, and re-layouts  2.47 us

profile of v3, /device:TPU:1, one launch (start us, length us, event | category | flops | bytes accessed | tf_op | source)
XLA Modules:
  0.0 106.5 jit_solution(5667509976538946007)
XLA Ops:
  0.6 103.4 %cholesky_qr.1 = (f32[48,2048]{1,0:T(8,128)}, f32[48,768]{1,0:T(8,128)}) custom-call(f32[48,2048]{1,0:T(8,128)} %s_hbm.1, f32[48,2048]{1,0:T(8,128)} %a_hbm.1), custom_call_target="tpu_custom_call" | custom-call | tf_op jit(solution)/shard_map/cholesky_qr/pallas_call | solution.py:458
  104.0 0.0 copy-start
  104.1 1.8 %copy.6 = f32[48,2048]{1,0:T(8,128)} copy(f32[48,2048]{1,0:T(8,128)} %get-tuple-element.4) | data formatting | bytes 786432
  105.9 0.0 copy-done
  105.9 0.7 copy.7
Async XLA Ops:
  104.0 1.8 %copy-start = (f32[48,768]{1,0:T(8,128)S(1)}, f32[48,768]{1,0:T(8,128)}, u32[]{:S(2)}) copy-start(f32[48,768]{1,0:T(8,128)} %get-tuple-element.5) | copy-start | bytes 442372
